TPU v7x, 256 devices: a 8x8x2 block of a 8x8x16 slice. The times are simulated.
256 devices in a mesh: groups: 2 (over z), seq: 128 (over x, y, core).
Axes of the slice: x: 8, y: 8, z: 2, core: 2. Of those that a mesh axis runs over, the one named last changes fastest.
The devices are a block of a 8x8x16 slice.
Arguments:
- latents: bfloat16 [2048, 64, 640], P(('groups', 'seq')), parts along dimension 0, may hold values from -6 to 6
- norm_gain: float32 [640], replicated, may hold values from 0.25 to 1.75
- norm_bias: float32 [640], replicated, may hold values from -3 to 3
- conv_weight: bfloat16 [5760, 640], P('seq'), may hold values from -0.078125 to 0.078125
- time_weight: bfloat16 [320, 640], replicated, may hold values from -0.3125 to 0.3125
- first_gain: float32 [640], replicated, may hold values from 0.25 to 1.75
- tconv_weight: bfloat16 [1920, 640], P('seq'), may hold values from -0.125 to 0.125
- second_gain: float32 [640], replicated, may hold values from 0.25 to 1.75
- qkv_weight: bfloat16 [640, 1920], P('seq'), may hold values from -0.25 to 0.25
- out_weight: bfloat16 [640, 640], P('seq'), may hold values from -0.25 to 0.25
- timesteps: int32 [8], P('groups'), parts along dimension 0, may hold values from 0 to 999
Outputs:
- mixed: bfloat16 [2048, 64, 640], P(('groups', 'seq')), parts along dimension 0
There are 2 independent parts, one for each index of `groups`. A program takes and returns all parts, laid end to end along the dimension named above; an argument that names none is the same for every part. Nothing has to cross between parts.
All inputs are finite; a program needn't handle non-finite values.
Results may differ from a plain program's by a relative error of at most 0.008.
Values may be sent and summed in bfloat16 or wider, within the bound.
No kernel may reach another device: no remote copies, remote signals or barrier semaphores. Data moves between devices by JAX's collectives and lax.ppermute only.
A program may use at most 128 MiB of HBM per device.

v0:
```python
import functools
import jax
import jax.numpy as jnp
from jax import lax
from jax.sharding import Mesh
from jax.sharding import PartitionSpec as P

HEAD = 64
GROUPS = 32
TFEAT = 320
FRAMES = 16
SEQ = ("seq_0", "seq_1", "seq_2")
GROUPS_SEQ = ("groups", "seq_0", "seq_1", "seq_2")


def in_order(parts, dim):
    dims = list(parts.shape[1:])
    dims[dim] *= parts.shape[0]
    return jnp.moveaxis(parts, 0, dim).reshape(dims)


def one_gather(arrays, axis, dims):
    ravelled = jnp.concatenate([a.reshape(-1) for a in arrays])
    lines, at, gathered = (lax.all_gather(ravelled, axis), 0, [])
    for a, dim in zip(arrays, dims):
        parts = lines[:, at : at + a.size].reshape(-1, *a.shape)
        gathered.append(in_order(parts, dim))
        at += a.size
    return tuple(gathered)


def one_axis_at_a_time(shard, axes):
    return functools.reduce(lax.psum, axes, shard)


def from_behind(block, axis, distance):
    devices = range(lax.axis_size(axis))
    route = [(i - distance, i) for i in devices if i - distance in devices]
    return lax.ppermute(block, axis, route)


def time_embed(timesteps, time_weight):
    half = TFEAT // 2
    freqs = jnp.exp(-jnp.log(10000.0) * jnp.arange(half, dtype=jnp.float32) / half)
    angles = timesteps.astype(jnp.float32)[:, None] * freqs[None, :]
    feats = jnp.concatenate([jnp.cos(angles), jnp.sin(angles)], axis=-1)
    return jnp.dot(feats, time_weight.astype(jnp.float32))


def layer_norm(values):
    mean = jnp.mean(values, axis=-1, keepdims=True)
    centered = values - mean
    var = jnp.mean(centered * centered, axis=-1, keepdims=True)
    return centered * lax.rsqrt(var + 1e-05)


def temporal_block(spatial, first_gain, tconv_weight, second_gain, qkv_weight, out_weight):
    clips, frames, places, chans = spatial.shape
    heads = chans // HEAD
    values = spatial.astype(jnp.float32)
    first = (layer_norm(values) * first_gain).astype(jnp.bfloat16)
    zero = jnp.zeros_like(first[:, :1])
    before = jnp.concatenate([zero, first[:, :-1]], axis=1)
    after = jnp.concatenate([first[:, 1:], zero], axis=1)
    stacked = jnp.concatenate([before, first, after], axis=-1).reshape(-1, 3 * chans)
    mid = values + jnp.dot(stacked, tconv_weight, preferred_element_type=jnp.float32).reshape(
        values.shape
    )
    second = (layer_norm(mid) * second_gain).astype(jnp.bfloat16)
    qkv = jnp.dot(second.reshape(-1, chans), qkv_weight, preferred_element_type=jnp.float32).astype(
        jnp.bfloat16
    )
    qkv = qkv.reshape(clips, frames, places, 3, heads, HEAD)
    query, key, value = (qkv[:, :, :, 0], qkv[:, :, :, 1], qkv[:, :, :, 2])
    scores = jnp.einsum(
        "cfphd,cgphd->cphfg", query, key, preferred_element_type=jnp.float32
    ) * HEAD ** (-0.5)
    weights = jax.nn.softmax(scores, axis=-1).astype(jnp.bfloat16)
    attended = jnp.einsum(
        "cphfg,cgphd->cfphd", weights, value, preferred_element_type=jnp.float32
    ).astype(jnp.bfloat16)
    projected = jnp.dot(attended.reshape(-1, chans), out_weight, preferred_element_type=jnp.float32)
    return (mid + projected.reshape(mid.shape)).astype(jnp.bfloat16)


def shards(
    latents,
    norm_gain,
    norm_bias,
    conv_weight,
    time_weight,
    first_gain,
    tconv_weight,
    second_gain,
    qkv_weight,
    out_weight,
    timesteps,
):
    devices = lax.axis_size(SEQ)
    device = lax.axis_index(SEQ)
    clips = timesteps.shape[0]
    images = clips * FRAMES
    sharing = devices // images
    rows, width, chans = latents.shape
    height = sharing * rows
    image = device % images
    clip = image // FRAMES
    tconv_full, qkv_full, out_full = one_gather(
        (tconv_weight, qkv_weight, out_weight), SEQ, (0, 0, 0)
    )
    temb_all = time_embed(timesteps, time_weight)
    pick = (jnp.arange(clips) == clip).astype(jnp.float32)
    temb = jnp.sum(pick[:, None] * temb_all, axis=0)
    values = latents.astype(jnp.float32).reshape(rows * width, GROUPS, chans // GROUPS)
    partial_sums = jnp.stack([jnp.sum(values, axis=(0, 2)), jnp.sum(values * values, axis=(0, 2))])
    owner = (jnp.arange(images) == image).astype(jnp.float32)
    table = one_axis_at_a_time(owner[:, None, None] * partial_sums[None], SEQ)
    mine = jnp.sum(owner[:, None, None] * table, axis=0)
    entries = height * width * (chans // GROUPS)
    mean = mine[0] / entries
    var = mine[1] / entries - mean * mean
    normed = (values - mean[None, :, None]) * lax.rsqrt(var + 1e-05)[None, :, None]
    normed = normed.reshape(rows, width, chans) * norm_gain + norm_bias
    normed = jax.nn.silu(normed).astype(jnp.bfloat16)
    upper_rim = from_behind(normed[rows - 1 :], SEQ, images)
    lower_rim = from_behind(normed[:1], SEQ, -images)
    padded = jnp.concatenate([upper_rim, normed, lower_rim], axis=0)
    padded = jnp.pad(padded, ((0, 0), (1, 1), (0, 0)))
    taps = [padded[dy : dy + rows, dx : dx + width] for dy in range(3) for dx in range(3)]
    columns = jnp.concatenate(taps, axis=-1).reshape(rows * width, 9 * chans)
    base = latents.reshape(rows * width, chans).astype(jnp.float32) + temb[None, :]
    conv = jnp.dot(
        columns,
        lax.all_gather(conv_weight, SEQ, axis=0, tiled=True),
        preferred_element_type=jnp.float32,
    )
    spatial = (base + conv).astype(jnp.bfloat16)
    moved = lax.all_to_all(spatial, SEQ, split_axis=0, concat_axis=0, tiled=True)
    block = rows * width // devices
    places = sharing * block
    ordered = jnp.transpose(moved.reshape(sharing, clips, FRAMES, block, chans), (1, 2, 0, 3, 4))
    grouped = ordered.reshape(clips, FRAMES, places, chans)
    result = temporal_block(grouped, first_gain, tconv_full, second_gain, qkv_full, out_full)
    unordered = jnp.transpose(result.reshape(clips, FRAMES, sharing, block, chans), (2, 0, 1, 3, 4))
    returned = lax.all_to_all(
        unordered.reshape(rows * width, chans), SEQ, split_axis=0, concat_axis=0, tiled=True
    )
    return returned.reshape(rows, width, chans)


def solution(mesh):
    torus = Mesh(
        mesh.devices.reshape(mesh.shape["groups"], 8, 8, 2), ("groups", "seq_0", "seq_1", "seq_2")
    )
    return jax.shard_map(
        shards,
        mesh=torus,
        in_specs=(
            P(GROUPS_SEQ, None, None),
            P(),
            P(),
            P(SEQ, None),
            P(),
            P(),
            P(SEQ, None),
            P(),
            P(SEQ, None),
            P(SEQ, None),
            P("groups"),
        ),
        out_specs=P(GROUPS_SEQ, None, None),
        check_vma=False,
    )
```

profile of v0, /device:TPU:513, one launch (start us, length us, event | category | flops | bytes accessed | tf_op | source)
XLA Modules:
  0.0 346.2 jit_solution(1874407834715782001)
XLA Ops:
  12.4 24.3 %psum.21 = f32[64,2,32]{0,2,1:T(8,128)S(1)} all-reduce(f32[64,2,32]{0,2,1:T(8,128)S(1)} %broadcast_multiply_fusion.1), channel_id=1, replica_groups=mesh['groups'=2,'seq_0'=8,'seq_1'=8,'seq_2'=2] {'seq_0'}, use_global_device_ids=true, to_apply=%region_5.6 | all-reduce | flops 4096 | bytes 32768 | tf_op jit(solution)/shard_map/psum | solution.py:33
  36.7 33.6 %psum.22 = f32[64,2,32]{0,2,1:T(8,128)S(1)} all-reduce(f32[64,2,32]{0,2,1:T(8,128)S(1)} %psum.21), channel_id=1, replica_groups=mesh['groups'=2,'seq_0'=8,'seq_1'=8,'seq_2'=2] {'seq_1'}, use_global_device_ids=true, to_apply=%region_6.7 | all-reduce | flops 4096 | bytes 32768 | tf_op jit(solution)/shard_map/psum | solution.py:33
  70.3 20.2 %psum.23 = f32[64,2,32]{0,2,1:T(8,128)S(1)} all-reduce(f32[64,2,32]{0,2,1:T(8,128)S(1)} %psum.22), channel_id=1, replica_groups=mesh['groups'=2,'seq_0'=8,'seq_1'=8,'seq_2'=2] {'seq_2'}, use_global_device_ids=true, to_apply=%region_7.8 | all-reduce | flops 4096 | bytes 32768 | tf_op jit(solution)/shard_map/psum | solution.py:33
  92.2 2.6 collective-permute-start
  94.8 1.3 collective-permute-start.1
  96.6 1.9 collective-permute-done
  98.5 9.0 %collective-permute-done.1 = bf16[1,64,640]{2,1,0:T(8,128)(2,1)S(1)} collective-permute-done((bf16[1,64,640]{2,1,0:T(8,128)(2,1)S(1)}, bf16[1,64,640]{2,1,0:T(8,128)(2,1)S(1)}, u32[]{:S(2)}, u32[]{:S(2)}) %collective-permute-start.1) | collective-permute-done | bytes 81952 | tf_op jit(solution)/shard_map/ppermute | solution.py:39
  111.7 1.3 constant_dynamic-update-slice_fusion
  117.1 2.4 all-gather.8.cloned.1.call-done
  119.6 4.9 %copy.139 = bf16[128,1,22400]{2,0,1:T(8,128)(2,1)S(1)} copy(bf16[128,1,22400]{2,1,0:T(2,128)(2,1)} %all-gather.8.cloned.1.call-done) | data formatting | bytes 11468800
  124.4 2.4 copy-done.2
  126.9 76.5 %all-gather.6.cloned.1.call-done = bf16[128,45,640]{2,1,0:T(8,128)(2,1)} async-done(((bf16[1,45,640]{2,1,0:T(8,128)(2,1)}), bf16[128,45,640]{2,1,0:T(8,128)(2,1)}) %all-gather.6.cloned.1.call-update) | async-done | bytes 7372816 | tf_op jit(solution)/shard_map/all_gather | solution.py:134
  203.5 9.3 %reshape.157 = bf16[5760,640]{1,0:T(8,128)(2,1)} reshape(bf16[128,45,640]{2,1,0:T(8,128)(2,1)} %all-gather.6.cloned.1.call-done) | data formatting | bytes 14745600
  212.8 9.6 %fusion.24 = bf16[512,640]{1,0:T(8,128)(2,1)S(1)} fusion(f32[512,640]{1,0:T(8,128)S(1)} %bitcast_add_fusion, bf16[512,5760]{1,0:T(8,128)(2,1)} %bitcast.5, bf16[5760,640]{1,0:T(8,128)(2,1)} %reshape.157), kind=kOutput, calls=%fused_computation.28 | convolution fusion | flops 3775528960 | bytes 15237120 | tf_op jit(solution)/shard_map/dot_general | solution.py:132
  223.4 11.5 %all-to-all-start = ((bf16[128,4,640]{2,1,0:T(4,128)(2,1)}), bf16[128,4,640]{2,1,0:T(4,128)(2,1)}, u32[]{:S(2)}, u32[]{:S(2)}) async-start(bf16[128,4,640]{2,1,0:T(4,128)(2,1)} %all_to_all.12), calls=%async_computation | async-start | bytes 1310720 | tf_op jit(solution)/shard_map/all_to_all | solution.py:138
  234.9 4.2 %fusion.54 = (bf16[128,9600]{1,0:T(8,128)(2,1)S(1)}, bf16[128,9600]{1,0:T(8,128)(2,1)}) fusion(bf16[128,22400]{1,0:T(8,128)(2,1)} %bitcast.64), kind=kLoop, calls=%fused_computation.95 | loop fusion | bytes 9830400 | tf_op jit(solution)/shard_map/slice | solution.py:26
  239.1 6.1 %reshape.161 = bf16[1920,640,1,1]{1,0,2,3:T(8,128)(2,1)} reshape(bf16[128,9600]{1,0:T(8,128)(2,1)} %get-tuple-element.11) | data formatting | bytes 4915200 | tf_op jit(solution)/shard_map/reshape;reshape | solution.py:19
  245.1 3.5 %reshape_reshape.10 = bf16[640,1920]{1,0:T(8,128)(2,1)} reshape(bf16[128,9600]{1,0:T(8,128)(2,1)S(1)} %get-tuple-element.10) | data formatting | bytes 4915200 | tf_op jit(solution)/shard_map/reshape;reshape | solution.py:19
  249.2 7.5 %all-to-all-done = bf16[128,4,640]{2,1,0:T(4,128)(2,1)} async-done(((bf16[128,4,640]{2,1,0:T(4,128)(2,1)}), bf16[128,4,640]{2,1,0:T(4,128)(2,1)}, u32[]{:S(2)}, u32[]{:S(2)}) %all-to-all-start) | async-done | bytes 655392 | tf_op jit(solution)/shard_map/all_to_all | solution.py:138
  258.6 1.9 copy.98
  260.5 1.7 reshape.152
  264.4 3.2 fusion.58
  269.4 3.0 convolution_convert_fusion
  272.4 7.5 %reshape.148 = bf16[4,16,8,3,10,64]{5,4,3,2,1,0:T(8,128)(2,1)} reshape(bf16[512,1920]{1,0:T(8,128)(2,1)} %convolution_convert_fusion) | data formatting | bytes 3932160 | tf_op jit(solution)/shard_map/reshape | solution.py:73
  279.9 5.6 %fusion.53 = (bf16[4,16,8,1,10,64]{5,4,3,2,1,0:T(8,128)(2,1)S(1)}, bf16[4,16,8,1,10,64]{5,4,3,2,1,0:T(8,128)(2,1)S(1)}, bf16[4,16,8,1,10,64]{5,4,3,2,1,0:T(8,128)(2,1)S(1)}) fusion(bf16[4,16,8,3,10,64]{5,4,3,2,1,0:T(8,128)(2,1)} %reshape.148), kind=kLoop, calls=%fused_computation.94 | loop fusion | bytes 3932160 | tf_op jit(solution)/shard_map/slice | solution.py:74
  285.5 1.6 fusion.26
  287.1 11.1 %fusion.59 = (f32[4,8,10,16]{3,2,1,0:T(8,128)S(1)}, f32[4,8,10,16,16]{3,4,2,1,0:T(8,128)S(1)}) fusion(f32[4,8,10,16,16]{3,4,2,1,0:T(8,128)S(1)} %fusion.26), kind=kOutput, calls=%fused_computation.100 | output fusion | flops 327695 | bytes 675840 | tf_op jit(solution)/shard_map/sub | solution.py:78
  299.3 1.9 copy.110
  301.3 3.0 dot_general.29
  304.2 1.6 fusion.25
  305.8 1.6 reshape.149
  308.0 30.4 %all_to_all.18 = bf16[128,4,640]{2,1,0:T(4,128)(2,1)S(1)} all-to-all(bf16[128,4,640]{2,1,0:T(4,128)(2,1)S(1)} %copy.112), channel_id=1, replica_groups=mesh['groups'=2,'seq_0'=8,'seq_1'=8,'seq_2'=2] {'seq_0','seq_1','seq_2'}, dimensions={0} | all-to-all | bytes 1310720 | tf_op jit(solution)/shard_map/all_to_all | solution.py:145
  (85 shorter events, 26.0 us)
Async XLA Ops:
  6.5 89.8 %copy-start = (bf16[320,640]{1,0:T(8,128)(2,1)S(1)}, bf16[320,640]{1,0:T(8,128)(2,1)}, u32[]{:S(2)}) copy-start(bf16[320,640]{1,0:T(8,128)(2,1)} %param.15) | copy-start | bytes 1228804
  6.6 84.5 %copy-start.3 = (bf16[8,64,640]{2,1,0:T(8,128)(2,1)S(1)}, bf16[8,64,640]{2,1,0:T(8,128)(2,1)}, u32[]{:S(2)}) copy-start(bf16[8,64,640]{2,1,0:T(8,128)(2,1)} %param.11) | copy-start | bytes 1966084
  6.6 89.6 %copy-start.11 = (s32[4]{0:T(128)S(1)}, s32[4]{0:T(128)}, u32[]{:S(2)}) copy-start(s32[4]{0:T(128)} %param.21) | copy-start | bytes 52
  6.6 113.0 %all-gather.8.cloned.1.call-start = ((), (), s32[]{:S(2)}) async-start(), calls=%async_computation.3 | async-start | bytes 11558400 | tf_op jit(solution)/shard_map/all_gather | solution.py:24
  9.7 193.8 %all-gather.6.cloned.1.call-start = ((), (), s32[]{:S(2)}) async-start(), calls=%async_computation.2 | async-start | bytes 7925760 | tf_op jit(solution)/shard_map/all_gather | solution.py:134
  92.2 6.3 %collective-permute-start = (bf16[1,64,640]{2,1,0:T(8,128)(2,1)S(1)}, bf16[1,64,640]{2,1,0:T(8,128)(2,1)S(1)}, u32[]{:S(2)}, u32[]{:S(2)}) collective-permute-start(bf16[1,64,640]{2,1,0:T(8,128)(2,1)S(1)} %get-tuple-element.16), channel_id=1, source_target_pairs={{0,64},{1,65},{2,66},{3,67},{4,68},{5,69},{6,70},{7,71},{8,72},{9,... | collective-permute-start | bytes 245768 | tf_op jit(solution)/shard_map/ppermute | solution.py:39
  94.8 12.8 %collective-permute-start.1 = (bf16[1,64,640]{2,1,0:T(8,128)(2,1)S(1)}, bf16[1,64,640]{2,1,0:T(8,128)(2,1)S(1)}, u32[]{:S(2)}, u32[]{:S(2)}) collective-permute-start(bf16[1,64,640]{2,1,0:T(8,128)(2,1)S(1)} %get-tuple-element.17), channel_id=1, source_target_pairs={{64,0},{65,1},{66,2},{67,3},{68,4},{69,5},{70,6},{71,7},{72,8},{73... | collective-permute-start | bytes 245768 | tf_op jit(solution)/shard_map/ppermute | solution.py:39
  108.8 2.9 copy-start.7
  108.8 2.9 copy-start.8
  124.4 2.4 copy-start.2
  223.4 33.3 %all-to-all-start = ((bf16[128,4,640]{2,1,0:T(4,128)(2,1)}), bf16[128,4,640]{2,1,0:T(4,128)(2,1)}, u32[]{:S(2)}, u32[]{:S(2)}) async-start(bf16[128,4,640]{2,1,0:T(4,128)(2,1)} %all_to_all.12), calls=%async_computation | async-start | bytes 1310720 | tf_op jit(solution)/shard_map/all_to_all | solution.py:138
  260.5 1.8 copy-start.9
  262.3 1.1 copy-start.4
  262.3 2.1 copy-start.6
  264.4 3.6 %copy-start.10 = (f32[640]{0:T(1024)S(1)}, f32[640]{0:T(1024)}, u32[]{:S(2)}) copy-start(f32[640]{0:T(1024)} %param.18) | copy-start | bytes 7684
  267.7 1.7 copy-start.5
  307.5 31.9 %copy-start.1 = (bf16[320,640]{1,0:T(8,128)(2,1)S(1)}, bf16[320,640]{1,0:T(8,128)(2,1)}, u32[]{:S(2)}) copy-start(bf16[320,640]{1,0:T(8,128)(2,1)} %param.15) | copy-start | bytes 1228804
Sparse Core Ops, SparseCore 0:
  10.0 109.5 all-gather.7
  122.2 81.2 all-gather.5
where the time goes:
time: 348 us; the launch traced here: 346 us
  blocking collectives  109 us (31%)
  waiting for transfers between devices  98.1 us (28%)
  local copies, waits for them, and re-layouts  69.6 us (20%)
  matrix products  20.4 us (6%)
  other arithmetic  20.3 us (6%)
  starting transfers between devices  15.4 us (4%)
  between operations  13.9 us (4%)
    psum x3, blocking collectives, one_axis_at_a_time(): return functools.reduce(lax.psum, axes, shard)  78.2 us
    all_gather x1, waiting for transfers between devices, shards(): lax.all_gather(conv_weight, SEQ, axis=0, tiled=True)  76.5 us
    all_to_all x1, blocking collectives, shards(): lax.all_to_all(unordered.reshape(rows * width, chans), SEQ, split_axis=0,...  30.4 us
    unnamed x32, local copies, waits for them, and re-layouts  25.2 us
    all_to_all x1, starting transfers between devices, shards(): lax.all_to_all(spatial, SEQ, split_axis=0, concat_axis=0, tiled=True)  11.5 us
    sub x1, other arithmetic, temporal_block(): weights = jax.nn.softmax(scores, axis=-1).astype(jnp.bfloat16)  11.1 us
    ppermute x2, waiting for transfers between devices, from_behind(): return lax.ppermute(block, axis, route)  10.9 us
    another operation x3, local copies, waits for them, and re-layouts, in_order(): return jnp.moveaxis(parts, 0, dim).reshape(dims)  10.1 us
  transfers between devices with their start and end apart: 5, of which 5 were waited for; matrix products, arithmetic and copies ran while one was open for 9% of the time, Pallas kernels for 0%

commit v1 on v0

--- a/solution.py
+++ b/solution.py
@@ -131,7 +131,9 @@
     base = latents.reshape(rows * width, chans).astype(jnp.float32) + temb[None, :]
     conv = jnp.dot(
         columns,
-        lax.all_gather(conv_weight, SEQ, axis=0, tiled=True),
+        jnp.concatenate(
+            lax.all_to_all(jnp.stack([conv_weight] * lax.axis_size(SEQ)), SEQ, 0, 0), axis=0
+        ),
         preferred_element_type=jnp.float32,
     )
     spatial = (base + conv).astype(jnp.bfloat16)

time: 348 us -> 492 us (1.41); the launches traced: 346 us -> 485 us
  blocking collectives: 109 us -> 301 us
  waiting for transfers between devices: 98.1 us -> 12.5 us
  starting transfers between devices: 15.4 us -> 46.2 us
    psum x3, blocking collectives: 78.2 us -> 269 us  [one_axis_at_a_time(): return functools.reduce(lax.psum, axes, shard)]
    all_gather x1 -> x0, waiting for transfers between devices: 76.5 us -> none  [shards(): lax.all_gather(conv_weight, SEQ, axis=0, tiled=True)]
    all_to_all x0 -> x1, starting transfers between devices: none -> 28.4 us  [shards(): lax.all_to_all(jnp.stack([conv_weight] * lax.axis_size(SEQ)), SEQ, 0, 0)]
    unnamed x32 -> x37, local copies, waits for them, and re-layouts: 25.2 us -> 15.6 us
    reshape x0 -> x1, local copies, waits for them, and re-layouts: none -> 9.3 us  [shards(): jnp.concatenate(lax.all_to_all(jnp.stack([conv_weight] * lax.axis_size(SE...]
  transfers between devices with their start and end apart: 5 -> 5, of which waited for: 5 -> 2; matrix products, arithmetic and copies ran while one was open for 9% -> 7% of each run, Pallas kernels for 0% -> 0%
where the time goes in v1:
time: 492 us; the launch traced here: 485 us
  blocking collectives  301 us (61%)
  local copies, waits for them, and re-layouts  74 us (15%)
  starting transfers between devices  46.2 us (9%)
  matrix products  19.4 us (4%)
  other arithmetic  17.4 us (4%)
  between operations  14.2 us (3%)
  waiting for transfers between devices  12.5 us (3%)
    psum x3, blocking collectives, one_axis_at_a_time(): return functools.reduce(lax.psum, axes, shard)  269 us
    all_to_all x1, blocking collectives, shards(): lax.all_to_all(unordered.reshape(rows * width, chans), SEQ, split_axis=0,...  32.5 us
    all_to_all x1, starting transfers between devices, shards(): lax.all_to_all(jnp.stack([conv_weight] * lax.axis_size(SEQ)), SEQ, 0, 0)  28.4 us
    unnamed x37, local copies, waits for them, and re-layouts  15.6 us
    another operation x3, local copies, waits for them, and re-layouts, in_order(): return jnp.moveaxis(parts, 0, dim).reshape(dims)  11.9 us
    sub x1, other arithmetic, temporal_block(): weights = jax.nn.softmax(scores, axis=-1).astype(jnp.bfloat16)  11.1 us
  transfers between devices with their start and end apart: 5, of which 2 were waited for; matrix products, arithmetic and copies ran while one was open for 7% of the time, Pallas kernels for 0%

profile of v1, /device:TPU:513, one launch (start us, length us, event | category | flops | bytes accessed | tf_op | source)
XLA Modules:
  0.0 485.1 jit_solution(3630735884650847232)
XLA Ops:
  6.6 4.6 stack.11
  11.2 28.4 %all-to-all-start = ((bf16[128,45,640]{2,1,0:T(8,128)(2,1)}), bf16[128,45,640]{2,1,0:T(8,128)(2,1)}, u32[]{:S(2)}, u32[]{:S(2)}) async-start(bf16[128,45,640]{2,1,0:T(8,128)(2,1)} %stack.11), calls=%async_computation | async-start | bytes 15728640 | tf_op jit(solution)/shard_map/all_to_all | solution.py:135
  41.4 232.4 %psum.21 = f32[64,2,32]{0,2,1:T(8,128)S(1)} all-reduce(f32[64,2,32]{0,2,1:T(8,128)S(1)} %broadcast_multiply_fusion.1), channel_id=1, replica_groups=mesh['groups'=2,'seq_0'=8,'seq_1'=8,'seq_2'=2] {'seq_0'}, use_global_device_ids=true, to_apply=%region_5.6 | all-reduce | flops 4096 | bytes 32768 | tf_op jit(solution)/shard_map/psum | solution.py:33
  273.8 23.3 %psum.22 = f32[64,2,32]{0,2,1:T(8,128)S(1)} all-reduce(f32[64,2,32]{0,2,1:T(8,128)S(1)} %psum.21), channel_id=1, replica_groups=mesh['groups'=2,'seq_0'=8,'seq_1'=8,'seq_2'=2] {'seq_1'}, use_global_device_ids=true, to_apply=%region_6.7 | all-reduce | flops 4096 | bytes 32768 | tf_op jit(solution)/shard_map/psum | solution.py:33
  297.1 13.2 %psum.23 = f32[64,2,32]{0,2,1:T(8,128)S(1)} all-reduce(f32[64,2,32]{0,2,1:T(8,128)S(1)} %psum.22), channel_id=1, replica_groups=mesh['groups'=2,'seq_0'=8,'seq_1'=8,'seq_2'=2] {'seq_2'}, use_global_device_ids=true, to_apply=%region_7.8 | all-reduce | flops 4096 | bytes 32768 | tf_op jit(solution)/shard_map/psum | solution.py:33
  311.3 6.8 %collective-permute-start = (bf16[1,64,640]{2,1,0:T(8,128)(2,1)S(1)}, bf16[1,64,640]{2,1,0:T(8,128)(2,1)S(1)}, u32[]{:S(2)}, u32[]{:S(2)}) collective-permute-start(bf16[1,64,640]{2,1,0:T(8,128)(2,1)S(1)} %get-tuple-element.16), channel_id=1, source_target_pairs={{0,64},{1,65},{2,66},{3,67},{4,68},{5,69},{6,70},{7,71},{8,72},{9,... | collective-permute-start | bytes 245768 | tf_op jit(solution)/shard_map/ppermute | solution.py:39
  318.1 1.8 collective-permute-start.1
  320.4 6.8 %collective-permute-done.1 = bf16[1,64,640]{2,1,0:T(8,128)(2,1)S(1)} collective-permute-done((bf16[1,64,640]{2,1,0:T(8,128)(2,1)S(1)}, bf16[1,64,640]{2,1,0:T(8,128)(2,1)S(1)}, u32[]{:S(2)}, u32[]{:S(2)}) %collective-permute-start.1) | collective-permute-done | bytes 81952 | tf_op jit(solution)/shard_map/ppermute | solution.py:39
  331.4 1.3 constant_dynamic-update-slice_fusion
  336.8 4.9 %copy.139 = bf16[128,1,22400]{2,0,1:T(8,128)(2,1)S(1)} copy(bf16[128,1,22400]{2,1,0:T(2,128)(2,1)} %all-gather.4.cloned.1.call-done) | data formatting | bytes 11468800
  341.7 2.5 copy-done.2
  345.2 9.3 %reshape.149 = bf16[5760,640]{1,0:T(8,128)(2,1)} reshape(bf16[128,45,640]{2,1,0:T(8,128)(2,1)} %all-to-all-done) | data formatting | bytes 14745600 | tf_op jit(solution)/shard_map/reshape | solution.py:134
  354.5 9.6 %fusion.24 = bf16[512,640]{1,0:T(8,128)(2,1)S(1)} fusion(f32[512,640]{1,0:T(8,128)S(1)} %bitcast_add_fusion, bf16[512,5760]{1,0:T(8,128)(2,1)} %bitcast.5, bf16[5760,640]{1,0:T(8,128)(2,1)} %reshape.149), kind=kOutput, calls=%fused_computation.28 | convolution fusion | flops 3775528960 | bytes 15237120 | tf_op jit(solution)/shard_map/dot_general | solution.py:132
  365.1 9.2 %all-to-all-start.1 = ((bf16[128,4,640]{2,1,0:T(4,128)(2,1)}), bf16[128,4,640]{2,1,0:T(4,128)(2,1)S(1)}, u32[]{:S(2)}, u32[]{:S(2)}) async-start(bf16[128,4,640]{2,1,0:T(4,128)(2,1)} %all_to_all.16), calls=%async_computation.1 | async-start | bytes 1310720 | tf_op jit(solution)/shard_map/all_to_all | solution.py:140
  374.3 4.3 fusion.54
  378.6 6.1 %reshape.165 = bf16[1920,640,1,1]{1,0,2,3:T(8,128)(2,1)} reshape(bf16[128,9600]{1,0:T(8,128)(2,1)} %get-tuple-element.11) | data formatting | bytes 4915200 | tf_op jit(solution)/shard_map/reshape;reshape | solution.py:19
  384.6 3.5 reshape_reshape.10
  388.2 2.4 reshape.166
  390.5 5.7 %all-to-all-done.1 = bf16[128,4,640]{2,1,0:T(4,128)(2,1)S(1)} async-done(((bf16[128,4,640]{2,1,0:T(4,128)(2,1)}), bf16[128,4,640]{2,1,0:T(4,128)(2,1)S(1)}, u32[]{:S(2)}, u32[]{:S(2)}) %all-to-all-start.1) | async-done | bytes 655392 | tf_op jit(solution)/shard_map/all_to_all | solution.py:140
  397.0 1.9 copy.98
  398.9 1.7 reshape.158
  401.1 1.3 copy-done.6
  402.5 1.9 fusion.58
  406.1 3.1 convolution_convert_fusion
  409.2 7.7 %reshape.154 = bf16[4,16,8,3,10,64]{5,4,3,2,1,0:T(8,128)(2,1)} reshape(bf16[512,1920]{1,0:T(8,128)(2,1)} %convolution_convert_fusion) | data formatting | bytes 3932160 | tf_op jit(solution)/shard_map/reshape | solution.py:73
  416.9 5.6 %fusion.53 = (bf16[4,16,8,1,10,64]{5,4,3,2,1,0:T(8,128)(2,1)S(1)}, bf16[4,16,8,1,10,64]{5,4,3,2,1,0:T(8,128)(2,1)S(1)}, bf16[4,16,8,1,10,64]{5,4,3,2,1,0:T(8,128)(2,1)S(1)}) fusion(bf16[4,16,8,3,10,64]{5,4,3,2,1,0:T(8,128)(2,1)} %reshape.154), kind=kLoop, calls=%fused_computation.94 | loop fusion | bytes 3932160 | tf_op jit(solution)/shard_map/slice | solution.py:74
  422.4 1.6 fusion.26
  424.0 11.1 %fusion.59 = (f32[4,8,10,16]{3,2,1,0:T(8,128)S(1)}, f32[4,8,10,16,16]{3,4,2,1,0:T(8,128)S(1)}) fusion(f32[4,8,10,16,16]{3,4,2,1,0:T(8,128)S(1)} %fusion.26), kind=kOutput, calls=%fused_computation.100 | output fusion | flops 327695 | bytes 675840 | tf_op jit(solution)/shard_map/sub | solution.py:78
  436.2 1.9 copy.110
  438.1 3.8 dot_general.29
  441.9 1.8 fusion.25
  444.6 32.5 %all_to_all.23 = bf16[128,4,640]{2,1,0:T(4,128)(2,1)S(1)} all-to-all(bf16[128,4,640]{2,1,0:T(4,128)(2,1)S(1)} %copy.112), channel_id=1, replica_groups=mesh['groups'=2,'seq_0'=8,'seq_1'=8,'seq_2'=2] {'seq_0','seq_1','seq_2'}, dimensions={0} | all-to-all | bytes 1310720 | tf_op jit(solution)/shard_map/all_to_all | solution.py:147
  (91 shorter events, 18.9 us)
Async XLA Ops:
  6.5 313.5 %copy-start = (bf16[320,640]{1,0:T(8,128)(2,1)S(1)}, bf16[320,640]{1,0:T(8,128)(2,1)}, u32[]{:S(2)}) copy-start(bf16[320,640]{1,0:T(8,128)(2,1)} %param.15) | copy-start | bytes 1228804
  11.2 28.5 %copy-start.8 = (bf16[15,640]{1,0:T(8,128)(2,1)S(1)}, bf16[15,640]{1,0:T(8,128)(2,1)}, u32[]{:S(2)}) copy-start(bf16[15,640]{1,0:T(8,128)(2,1)} %param.17) | copy-start | bytes 57604
  11.2 28.6 %copy-start.7 = (bf16[5,1920]{1,0:T(8,128)(2,1)S(1)}, bf16[5,1920]{1,0:T(8,128)(2,1)}, u32[]{:S(2)}) copy-start(bf16[5,1920]{1,0:T(8,128)(2,1)} %param.19) | copy-start | bytes 57604
  11.2 28.6 %copy-start.11 = (bf16[5,640]{1,0:T(8,128)(2,1)S(1)}, bf16[5,640]{1,0:T(8,128)(2,1)}, u32[]{:S(2)}) copy-start(bf16[5,640]{1,0:T(8,128)(2,1)} %param.20) | copy-start | bytes 19204
  11.2 29.5 %copy-start.3 = (bf16[8,64,640]{2,1,0:T(8,128)(2,1)S(1)}, bf16[8,64,640]{2,1,0:T(8,128)(2,1)}, u32[]{:S(2)}) copy-start(bf16[8,64,640]{2,1,0:T(8,128)(2,1)} %param.11) | copy-start | bytes 1966084
  11.2 299.6 %copy-start.9 = (f32[640]{0:T(1024)S(1)}, f32[640]{0:T(1024)}, u32[]{:S(2)}) copy-start(f32[640]{0:T(1024)} %param.13) | copy-start | bytes 7684
  11.2 299.6 %copy-start.10 = (f32[640]{0:T(1024)S(1)}, f32[640]{0:T(1024)}, u32[]{:S(2)}) copy-start(f32[640]{0:T(1024)} %param.12) | copy-start | bytes 7684
  11.2 334.0 %all-to-all-start = ((bf16[128,45,640]{2,1,0:T(8,128)(2,1)}), bf16[128,45,640]{2,1,0:T(8,128)(2,1)}, u32[]{:S(2)}, u32[]{:S(2)}) async-start(bf16[128,45,640]{2,1,0:T(8,128)(2,1)} %stack.11), calls=%async_computation | async-start | bytes 15728640 | tf_op jit(solution)/shard_map/all_to_all | solution.py:135
  39.6 280.3 %copy-start.14 = (s32[4]{0:T(128)S(1)}, s32[4]{0:T(128)}, u32[]{:S(2)}) copy-start(s32[4]{0:T(128)} %param.21) | copy-start | bytes 52
  39.7 297.1 %all-gather.4.cloned.1.call-start = ((), (), s32[]{:S(2)}) async-start(), calls=%async_computation.3 | async-start | bytes 11558400 | tf_op jit(solution)/shard_map/all_gather | solution.py:24
  311.3 9.1 %collective-permute-start = (bf16[1,64,640]{2,1,0:T(8,128)(2,1)S(1)}, bf16[1,64,640]{2,1,0:T(8,128)(2,1)S(1)}, u32[]{:S(2)}, u32[]{:S(2)}) collective-permute-start(bf16[1,64,640]{2,1,0:T(8,128)(2,1)S(1)} %get-tuple-element.16), channel_id=1, source_target_pairs={{0,64},{1,65},{2,66},{3,67},{4,68},{5,69},{6,70},{7,71},{8,72},{9,... | collective-permute-start | bytes 245768 | tf_op jit(solution)/shard_map/ppermute | solution.py:39
  318.1 9.1 %collective-permute-start.1 = (bf16[1,64,640]{2,1,0:T(8,128)(2,1)S(1)}, bf16[1,64,640]{2,1,0:T(8,128)(2,1)S(1)}, u32[]{:S(2)}, u32[]{:S(2)}) collective-permute-start(bf16[1,64,640]{2,1,0:T(8,128)(2,1)S(1)} %get-tuple-element.17), channel_id=1, source_target_pairs={{64,0},{65,1},{66,2},{67,3},{68,4},{69,5},{70,6},{71,7},{72,8},{73... | collective-permute-start | bytes 245768 | tf_op jit(solution)/shard_map/ppermute | solution.py:39
  341.7 2.5 copy-start.2
  365.1 31.1 %all-to-all-start.1 = ((bf16[128,4,640]{2,1,0:T(4,128)(2,1)}), bf16[128,4,640]{2,1,0:T(4,128)(2,1)S(1)}, u32[]{:S(2)}, u32[]{:S(2)}) async-start(bf16[128,4,640]{2,1,0:T(4,128)(2,1)} %all_to_all.16), calls=%async_computation.1 | async-start | bytes 1310720 | tf_op jit(solution)/shard_map/all_to_all | solution.py:140
  398.9 1.8 copy-start.12
  400.8 1.7 copy-start.6
  402.5 2.2 copy-start.13
  404.4 1.7 copy-start.5
  438.1 3.8 copy-start.4
  444.0 34.0 %copy-start.1 = (bf16[320,640]{1,0:T(8,128)(2,1)S(1)}, bf16[320,640]{1,0:T(8,128)(2,1)}, u32[]{:S(2)}) copy-start(bf16[320,640]{1,0:T(8,128)(2,1)} %param.15) | copy-start | bytes 1228804
Sparse Core Ops, SparseCore 0:
  43.1 257.1 all-gather.3
